TPU v7x, 32 devices: a whole 2x2x4 slice. The times are simulated.
32 devices in a mesh: dp: 4 (over y, x), fsdp: 8 (over z, core).
Axes of the slice: x: 2, y: 2, z: 4, core: 2. Of those that a mesh axis runs over, the one named last changes fastest.
Arguments:
- hidden: bfloat16 [16384, 4096], P(('dp', 'fsdp')), may hold values from -6 to 6
- queries: bfloat16 [16384, 2048], P(('dp', 'fsdp')), may hold values from -60 to 60
- cotangent: bfloat16 [16384, 2048], P(('dp', 'fsdp')), may hold values from -0.125 to 0.125
- point_start: bfloat16 [4096, 1024], P('fsdp', 'dp'), may hold values from -0.09375 to 0.09375
- point_mid: bfloat16 [4096, 1024], P('fsdp', 'dp'), may hold values from -0.09375 to 0.09375
- point_end: bfloat16 [4096, 1024], P('fsdp', 'dp'), may hold values from -0.09375 to 0.09375
- curve_time: float32 [1], replicated, may hold values from 0.15 to 0.85
Outputs:
- context: bfloat16 [16384, 2048], P(('dp', 'fsdp'))
- gradient: float32 [4096, 1024], P('fsdp', 'dp')
All inputs are finite; a program needn't handle non-finite values.
Results may differ from a plain program's by a relative error of at most 0.0071.
Values may be sent and summed in bfloat16 or wider, within the bound.
A program may use at most 128 MiB of HBM per device.

v0:
```python
import math

import jax
import jax.numpy as jnp
from jax import lax
from jax.sharding import PartitionSpec as P

KVH = 4
HD = 128


def rope_tables(seq_len, head_dim):
    positions = jnp.arange(seq_len, dtype=jnp.float32)[:, None]
    halves_index = jnp.arange(head_dim // 2, dtype=jnp.float32)[None, :]
    inverse = jnp.exp(-(2.0 * halves_index / head_dim) * math.log(500000.0))
    angles = positions * inverse
    cosine = jnp.concatenate([jnp.cos(angles), jnp.cos(angles)], axis=1)
    sine_t = jnp.concatenate([jnp.sin(angles), jnp.sin(angles)], axis=1)
    return (cosine, sine_t)


def rotate(values_in):
    half_size = values_in.shape[-1] // 2
    return jnp.concatenate([-values_in[..., half_size:], values_in[..., :half_size]], axis=-1)


def rotate_back(values_in):
    half_size = values_in.shape[-1] // 2
    return jnp.concatenate([values_in[..., half_size:], -values_in[..., :half_size]], axis=-1)


def attend(kv_rows, query_rows, grad_rows, kv_heads, head_dim):
    seq_len = kv_rows.shape[0]
    kv_width = kv_heads * head_dim
    group_size = query_rows.shape[1] // kv_width
    width_head = group_size * head_dim
    cosine, sine_t = rope_tables(seq_len, head_dim)
    causal = jnp.arange(seq_len)[:, None] >= jnp.arange(seq_len)[None, :]
    score_scale = 1.0 / math.sqrt(head_dim)
    contexts = []
    key_grads = []
    value_grads = []
    for kv_head in range(kv_heads):
        keys_raw = kv_rows[:, kv_head * head_dim : (kv_head + 1) * head_dim].astype(jnp.float32)
        values_head = kv_rows[
            :, kv_width + kv_head * head_dim : kv_width + (kv_head + 1) * head_dim
        ]
        keys_head = (keys_raw * cosine + rotate(keys_raw) * sine_t).astype(jnp.bfloat16)
        query_head = query_rows[:, kv_head * width_head : (kv_head + 1) * width_head].reshape(
            seq_len, group_size, head_dim
        )
        grad_head = grad_rows[:, kv_head * width_head : (kv_head + 1) * width_head].reshape(
            seq_len, group_size, head_dim
        )
        scores = (
            jnp.einsum("sgd,td->gst", query_head, keys_head, preferred_element_type=jnp.float32)
            * score_scale
        )
        scores = jnp.where(causal[None], scores, -1e30)
        top_score = jnp.max(scores, axis=-1, keepdims=True)
        weights_exp = jnp.exp(scores - top_score)
        probs = weights_exp / jnp.sum(weights_exp, axis=-1, keepdims=True)
        probs_low = probs.astype(jnp.bfloat16)
        context_head = jnp.einsum(
            "gst,td->sgd", probs_low, values_head, preferred_element_type=jnp.float32
        ).astype(jnp.bfloat16)
        contexts.append(context_head.reshape(seq_len, width_head))
        prob_grad = jnp.einsum(
            "sgd,td->gst", grad_head, values_head, preferred_element_type=jnp.float32
        )
        value_grads.append(
            jnp.einsum("gst,sgd->td", probs_low, grad_head, preferred_element_type=jnp.float32)
        )
        score_grad = (
            probs * (prob_grad - jnp.sum(prob_grad * probs, axis=-1, keepdims=True)) * score_scale
        )
        score_low = score_grad.astype(jnp.bfloat16)
        rot_grad = jnp.einsum(
            "gst,sgd->td", score_low, query_head, preferred_element_type=jnp.float32
        )
        key_grads.append(rot_grad * cosine + rotate_back(rot_grad * sine_t))
    context_rows = jnp.concatenate(contexts, axis=1)
    kv_grad = jnp.concatenate(key_grads + value_grads, axis=1).astype(jnp.bfloat16)
    return (context_rows, kv_grad)


def local(hidden, queries, cotangent, point_start, point_mid, point_end, curve_time):
    t_value = curve_time[0]
    blended = (
        (1.0 - t_value) ** 2 * point_start.astype(jnp.float32)
        + 2.0 * t_value * (1.0 - t_value) * point_mid.astype(jnp.float32)
        + t_value**2 * point_end.astype(jnp.float32)
    ).astype(jnp.bfloat16)
    seq_len = hidden.shape[0]
    model_width = hidden.shape[1]
    fsdp_count = lax.axis_size("fsdp")
    data_count = lax.axis_size("dp")
    columns_full = lax.all_gather(blended, "dp", axis=1, tiled=True)
    window = hidden
    kv_sum = jnp.dot(
        window,
        lax.all_gather(columns_full, "fsdp", axis=0, tiled=True),
        preferred_element_type=jnp.float32,
    )
    kv_rows = kv_sum.astype(jnp.bfloat16)
    context, kv_grad = attend(kv_rows, queries, cotangent, KVH, HD)
    bernstein = 2.0 * t_value * (1.0 - t_value)
    block_rows = model_width // (fsdp_count * data_count)
    permuted = (
        hidden.reshape(seq_len, fsdp_count, data_count, block_rows)
        .transpose(0, 2, 1, 3)
        .reshape(seq_len, model_width)
    )
    window = permuted
    joint_part = lax.psum_scatter(
        jnp.dot(window.T, kv_grad, preferred_element_type=jnp.float32),
        ("dp", "fsdp"),
        scatter_dimension=0,
        tiled=True,
    )
    gradient = lax.all_to_all(joint_part, "dp", split_axis=1, concat_axis=0, tiled=True)
    return (context, gradient * bernstein)


def solution(mesh):
    return jax.shard_map(
        local,
        mesh=mesh,
        in_specs=(
            P(("dp", "fsdp"), None),
            P(("dp", "fsdp"), None),
            P(("dp", "fsdp"), None),
            P("fsdp", "dp"),
            P("fsdp", "dp"),
            P("fsdp", "dp"),
            P(),
        ),
        out_specs=(P(("dp", "fsdp"), None), P("fsdp", "dp")),
        check_vma=False,
    )
```

profile of v0, /device:TPU:0, one launch (start us, length us, event | category | flops | bytes accessed | tf_op | source)
XLA Modules:
  0.0 428.7 jit_solution(16054272968819988394)
XLA Ops:
  7.9 2.0 add_convert_fusion
  9.9 29.6 %all-gather.3.cloned.1.call-done = bf16[512,1024]{1,0:T(8,128)(2,1)} async-done(((bf16[512,256]{1,0:T(8,128)(2,1)}), bf16[512,1024]{1,0:T(8,128)(2,1)}) %all-gather.3.cloned.1.call-update) | async-done | bytes 1048592 | tf_op jit(solution)/shard_map/all_gather | solution.py:98
  39.6 2.8 fusion.159
  42.4 2.1 copy.150
  44.5 2.1 copy.152
  46.5 1.0 copy.151
  47.5 1.0 copy.153
  48.5 1.2 fusion.158
  49.8 1.4 copy.157
  51.6 1.3 copy.154
  52.8 6.5 %copy.111 = bf16[512,4096]{0,1:T(8,128)(2,1)} copy(bf16[512,4096]{1,0:T(8,128)(2,1)} %param.7) | data formatting | bytes 8388608 | tf_op args[0]
  59.3 4.7 %copy.112 = bf16[512,4,8,128]{0,3,2,1:T(8,128)(2,1)} copy(bf16[512,4,8,128]{0,3,1,2:T(8,128)(2,1)} %bitcast.287) | data formatting | bytes 8388608 | tf_op jit(solution)/shard_map/transpose | solution.py:111
  65.3 57.8 %all-gather.5.cloned.1.call-done = bf16[4096,1024]{1,0:T(8,128)(2,1)} async-done(((bf16[512,1024]{1,0:T(8,128)(2,1)}), bf16[4096,1024]{1,0:T(8,128)(2,1)}) %all-gather.5.cloned.1.call-update) | async-done | bytes 8388624 | tf_op jit(solution)/shard_map/all_gather | solution.py:102
  123.2 9.1 %fusion.44 = bf16[512,1024]{0,1:T(8,128)(2,1)S(1)} fusion(bf16[4096,1024]{1,0:T(8,128)(2,1)} %all-gather.5.cloned.1.call-done, bf16[512,4096]{1,0:T(8,128)(2,1)} %param.7), kind=kOutput, calls=%fused_computation.67 | convolution fusion | flops 4295491584 | bytes 13631488 | tf_op jit(solution)/shard_map/dot_general | solution.py:100
  132.4 2.8 fusion.138
  135.2 2.7 fusion.139
  137.9 2.7 fusion.140
  140.6 2.7 fusion.141
  144.0 0.8 fusion.86
  144.9 4.8 %fusion.164 = (f32[4,512]{1,0:T(4,128)S(1)}, f32[4,512,512]{1,2,0:T(8,128)}) fusion(pred[512,512]{0,1:T(8,128)(4,1)} %iota_compare_fusion, bf16[512,4,128]{0,2,1:T(8,128)(2,1)} %bitcast.297, bf16[512,128]{0,1:T(8,128)(2,1)} %get-tuple-element.13), kind=kOutput, calls=%fused_computation.199 | convolution fusion | flops 272630272 | bytes 5120000 | tf_op jit(solution)/shard_map/sub | solution.py:61
  149.6 1.8 fusion.82
  151.5 4.8 %fusion.174 = (f32[4,512]{1,0:T(4,128)S(1)}, f32[4,512,512]{1,2,0:T(8,128)}) fusion(pred[512,512]{0,1:T(8,128)(4,1)} %iota_compare_fusion, bf16[512,4,128]{0,2,1:T(8,128)(2,1)} %bitcast.303, bf16[512,128]{0,1:T(8,128)(2,1)} %get-tuple-element.11), kind=kOutput, calls=%fused_computation.201 | convolution fusion | flops 272630272 | bytes 5120000 | tf_op jit(solution)/shard_map/sub | solution.py:61
  156.3 5.6 %fusion.169 = (f32[4,512]{1,0:T(4,128)}, f32[4,512,512]{1,2,0:T(8,128)}) fusion(pred[512,512]{0,1:T(8,128)(4,1)} %iota_compare_fusion, bf16[512,4,128]{0,2,1:T(8,128)(2,1)} %bitcast.299, bf16[512,128]{0,1:T(8,128)(2,1)S(1)} %copy-done.3), kind=kOutput, calls=%fused_computation.200 | convolution fusion | flops 272630272 | bytes 5120000 | tf_op jit(solution)/shard_map/sub | solution.py:61
  161.9 4.8 %fusion.179 = (f32[4,512]{1,0:T(4,128)S(1)}, f32[4,512,512]{1,2,0:T(8,128)}) fusion(pred[512,512]{0,1:T(8,128)(4,1)} %iota_compare_fusion, bf16[512,4,128]{0,2,1:T(8,128)(2,1)} %bitcast.301, bf16[512,128]{0,1:T(8,128)(2,1)} %get-tuple-element.10), kind=kOutput, calls=%fused_computation.202 | convolution fusion | flops 272630272 | bytes 5120000 | tf_op jit(solution)/shard_map/sub | solution.py:61
  166.7 8.5 %fusion.48 = f32[512,128]{0,1:T(8,128)} fusion(bf16[512,4,128]{0,2,1:T(8,128)(2,1)} %bitcast.302, f32[512,512,4]{1,0,2:T(8,128)} %fusion.138, f32[4,512,512]{1,2,0:T(8,128)} %get-tuple-element.47, f32[4,512]{1,0:T(4,128)S(1)} %get-tuple-element.46), kind=kOutput, calls=%fused_computation.75 | convolution fusion | flops 275778048 | bytes 9183232 | tf_op jit(solution)/shard_map/gst,sgd->td/dot_general | solution.py:78
  175.2 8.5 %fusion.47 = f32[512,128]{0,1:T(8,128)} fusion(bf16[512,4,128]{0,2,1:T(8,128)(2,1)} %bitcast.304, f32[512,512,4]{1,0,2:T(8,128)} %fusion.139, f32[4,512,512]{1,2,0:T(8,128)} %get-tuple-element.45, f32[4,512]{1,0:T(4,128)S(1)} %get-tuple-element.44), kind=kOutput, calls=%fused_computation.74 | convolution fusion | flops 275778048 | bytes 9183232 | tf_op jit(solution)/shard_map/gst,sgd->td/dot_general | solution.py:78
  183.7 8.3 %fusion.46 = f32[512,128]{0,1:T(8,128)} fusion(bf16[512,4,128]{0,2,1:T(8,128)(2,1)} %bitcast.300, f32[512,512,4]{1,0,2:T(8,128)} %fusion.140, f32[4,512,512]{1,2,0:T(8,128)} %get-tuple-element.43, f32[4,512]{1,0:T(4,128)S(1)} %copy-done.10), kind=kOutput, calls=%fused_computation.73 | convolution fusion | flops 275778048 | bytes 9183232 | tf_op jit(solution)/shard_map/gst,sgd->td/dot_general | solution.py:78
  192.0 8.9 %fusion.97 = (f32[512,128]{0,1:T(8,128)}, f32[512,128]{0,1:T(8,128)}, f32[512,128]{0,1:T(8,128)}, f32[512,128]{0,1:T(8,128)}, f32[512,128]{0,1:T(8,128)}) fusion(f32[512,64]{0,1:T(8,128)S(1)} %get-tuple-element.38, f32[512,128]{0,1:T(8,128)} %fusion.48, f32[512,128]{0,1:T(8,128)} %fusion.47, f32[512,128]{0,1:T(8,128)} %fusion.46, ...), kind=kOutput, calls=%fused_computation.130 | convolution fusion | flops 276105728 | bytes 11149312 | tf_op jit(solution)/shard_map/gst,sgd->td/dot_general | solution.py:78
  201.0 1.1 fusion.160
  202.1 1.3 fusion.163
  203.4 1.0 fusion.162
  204.4 1.0 fusion.161
  205.4 1.0 fusion.107
  206.4 1.0 fusion.106
  207.4 1.0 fusion.105
  209.4 1.4 copy-done.6
  211.5 1.4 copy-done.8
  213.7 1.4 copy-done.4
  215.9 1.4 copy-done
  217.3 8.1 %convolution_bitcast_fusion = f32[4096,1024]{0,1:T(8,128)} fusion(bf16[512,1024]{0,1:T(8,128)(2,1)S(1)} %fusion.56, bf16[512,4096]{0,1:T(8,128)(2,1)S(1)} %bitcast.288), kind=kOutput, calls=%fused_computation.8 | convolution fusion | flops 4294967296 | bytes 22020096 | tf_op jit(solution)/shard_map/dot_general | solution.py:116
  225.5 2.8 convolution_convert_fusion.1
  229.4 2.1 copy-done.9
  232.0 178.7 %reduce-scatter.2.cloned.1.call-done = f32[128,1024]{0,1:T(8,128)} async-done(((f32[4096,1024]{0,1:T(8,128)}), f32[128,1024]{0,1:T(8,128)}) %reduce-scatter.2.cloned.1.call-update) | async-done | bytes 524304 | tf_op jit(solution)/shard_map/reduce_scatter | solution.py:115
  410.6 3.5 all-to-all-start
  414.1 3.4 convolution_convert_fusion.4
  418.2 1.3 copy.87
  419.5 1.6 pad_maximum_fusion
  421.1 1.0 copy.113
  (43 shorter events, 8.5 us)
Async XLA Ops:
  7.2 32.3 %all-gather.3.cloned.1.call-start = ((), (), s32[]{:S(2)}) async-start(), calls=%async_computation.2 | async-start | bytes 1310720 | tf_op jit(solution)/shard_map/all_gather | solution.py:98
  9.8 113.3 %all-gather.5.cloned.1.call-start = ((), (), s32[]{:S(2)}) async-start(), calls=%async_computation.3 | async-start | bytes 9437184 | tf_op jit(solution)/shard_map/all_gather | solution.py:102
  39.5 9.0 %copy-start.1 = (bf16[512,2048]{1,0:T(8,128)(2,1)S(1)}, bf16[512,2048]{1,0:T(8,128)(2,1)}, u32[]{:S(2)}) copy-start(bf16[512,2048]{1,0:T(8,128)(2,1)} %param.9) | copy-start | bytes 6291460
  39.5 371.1 %reduce-scatter.2.cloned.1.call-start = ((), (), s32[]{:S(2)}) async-start(), calls=%async_computation.4 | async-start | bytes 17301504 | tf_op jit(solution)/shard_map/reduce_scatter | solution.py:115
  151.5 4.8 %copy-start.3 = (bf16[512,128]{0,1:T(8,128)(2,1)S(1)}, bf16[512,128]{0,1:T(8,128)(2,1)}, u32[]{:S(2)}) copy-start(bf16[512,128]{0,1:T(8,128)(2,1)} %get-tuple-element.12) | copy-start | bytes 393220
  175.2 8.6 %copy-start.10 = (f32[4,512]{1,0:T(4,128)S(1)}, f32[4,512]{1,0:T(4,128)}, u32[]{:S(2)}) copy-start(f32[4,512]{1,0:T(4,128)} %get-tuple-element.42) | copy-start | bytes 24580
  200.9 7.5 %copy-start.2 = (f32[512,128]{0,1:T(8,128)S(1)}, f32[512,128]{0,1:T(8,128)}, u32[]{:S(2)}) copy-start(f32[512,128]{0,1:T(8,128)} %get-tuple-element.48) | copy-start | bytes 786436
  200.9 7.6 %copy-start.5 = (f32[4,512,512]{1,2,0:T(8,128)S(1)}, f32[4,512,512]{1,2,0:T(8,128)}, u32[]{:S(2)}) copy-start(f32[4,512,512]{1,2,0:T(8,128)} %get-tuple-element.47) | copy-start | bytes 12582916
  208.5 2.2 copy-start.6
  210.7 2.2 copy-start.8
  212.9 2.2 copy-start.4
  215.1 2.2 copy-start
  225.4 3.5 copy-start.7
  228.9 2.6 copy-start.9
  410.6 10.5 %all-to-all-start = ((f32[128,4,256]{0,2,1:T(8,128)}), f32[128,4,256]{0,2,1:T(8,128)S(1)}, u32[]{:S(2)}, u32[]{:S(2)}) async-start(f32[128,4,256]{0,2,1:T(8,128)} %bitcast.305), calls=%async_computation.1 | async-start | bytes 1048576 | tf_op jit(solution)/shard_map/all_to_all | solution.py:121
Sparse Core Ops, SparseCore 0:
  10.4 29.0 all-gather.2
  41.1 82.0 all-gather.4
  225.6 185.0 reduce-scatter.1
where the time goes:
time: 430 us; the launch traced here: 429 us
  waiting for transfers between devices  266 us (62%)
  matrix products  92.8 us (22%)
  local copies, waits for them, and re-layouts  35.4 us (8%)
  other arithmetic  16.1 us (4%)
  between operations  14.6 us (3%)
    reduce_scatter x1, waiting for transfers between devices, local(): lax.psum_scatter(jnp.dot(window.T, kv_grad, preferred_element_type=jnp.fl...  179 us
    all_gather x1, waiting for transfers between devices, local(): lax.all_gather(columns_full, 'fsdp', axis=0, tiled=True)  57.8 us
    dot_general x4, matrix products, attend(): jnp.einsum('gst,sgd->td', score_low, query_head, preferred_element_type=j...  34.3 us
    all_gather x1, waiting for transfers between devices, local(): columns_full = lax.all_gather(blended, 'dp', axis=1, tiled=True)  29.6 us
    unnamed x31, local copies, waits for them, and re-layouts  23.8 us
    sub x4, matrix products, attend(): weights_exp = jnp.exp(scores - top_score)  20 us
    dot_general x4, matrix products, attend(): jnp.einsum('sgd,td->gst', grad_head, values_head, preferred_element_type=...  10.8 us
    dot_general x1, matrix products, local(): jnp.dot(window, lax.all_gather(columns_full, 'fsdp', axis=0, tiled=True),...  9.11 us
  transfers between devices with their start and end apart: 4, of which 3 were waited for; matrix products, arithmetic and copies ran while one was open for 8% of the time, Pallas kernels for 0%

commit v1 on v0

v1 whole, which is shorter than its diff:
```python
import functools
import math

import jax
import jax.numpy as jnp
from jax import lax
from jax.experimental import pallas as pl
from jax.experimental.pallas import tpu as pltpu
from jax.sharding import PartitionSpec as P

KVH = 4
HD = 128
BQ = 128
MESH = pl.DeviceIdType.MESH
VMEM_LIMIT = 60 * 1024 * 1024


def rope_tables(seq_len, head_dim):
    positions = jnp.arange(seq_len, dtype=jnp.float32)[:, None]
    halves_index = jnp.arange(head_dim // 2, dtype=jnp.float32)[None, :]
    inverse = jnp.exp(-(2.0 * halves_index / head_dim) * math.log(500000.0))
    angles = positions * inverse
    cosine = jnp.concatenate([jnp.cos(angles), jnp.cos(angles)], axis=1)
    sine_t = jnp.concatenate([jnp.sin(angles), jnp.sin(angles)], axis=1)
    return (cosine, sine_t)


def rotate(x):
    half = x.shape[-1] // 2
    return jnp.concatenate([-x[..., half:], x[..., :half]], axis=-1)


def rotate_back(x):
    half = x.shape[-1] // 2
    return jnp.concatenate([x[..., half:], -x[..., :half]], axis=-1)


NN = (((1,), (0,)), ((), ()))
NT = (((1,), (1,)), ((), ()))
TN = (((0,), (0,)), ((), ()))


def mm(x, y, dims=NN):
    return lax.dot_general(x, y, dims, preferred_element_type=jnp.float32)


def attend_kernel(k_ref, v_ref, q_ref, g_ref, cos_ref, sin_ref, ctx_ref, grad_ref, kg, vg):
    seq = k_ref.shape[0]
    group = q_ref.shape[1] // HD
    scale = 1.0 / math.sqrt(HD)
    to_base2 = scale * math.log2(math.e)
    raw = k_ref[...].astype(jnp.float32)
    cosine, sine_t = cos_ref[...], sin_ref[...]
    keys = (raw * cosine + rotate(raw) * sine_t).astype(jnp.bfloat16)
    values = v_ref[...]
    values_t = values.astype(jnp.float32).T.astype(jnp.bfloat16)
    kg[...] = jnp.zeros_like(kg)
    vg[...] = jnp.zeros_like(vg)
    for start in range(0, seq, BQ):
        nk = start + BQ
        rows = slice(start, nk)
        qs = jnp.concatenate([q_ref[rows, g * HD:(g + 1) * HD] for g in range(group)], axis=0)
        gs = jnp.concatenate([g_ref[rows, g * HD:(g + 1) * HD] for g in range(group)], axis=0)
        s = mm(keys[:nk], qs, NT)
        key_at = lax.broadcasted_iota(jnp.int32, (BQ, group * BQ), 0)
        query_at = lax.broadcasted_iota(jnp.int32, (BQ, group * BQ), 1) % BQ
        last = jnp.where(key_at <= query_at, s[start:], -1e30)
        s = last if start == 0 else jnp.concatenate([s[:start], last], axis=0)
        top = jnp.max(s, axis=0, keepdims=True)
        w = jnp.exp2((s - top) * to_base2)
        p = w * (1.0 / jnp.sum(w, axis=0, keepdims=True))
        p_low = p.astype(jnp.bfloat16)
        ctx_t = mm(values_t[:, :nk], p_low)
        dp = mm(values[:nk], gs, NT)
        vg[:nk] += mm(p_low, gs)
        delta = jnp.sum(dp * p, axis=0, keepdims=True)
        ds = (p * ((dp - delta) * scale)).astype(jnp.bfloat16)
        kg[:nk] += mm(ds, qs)
        ctx = ctx_t.T.astype(jnp.bfloat16)
        for g in range(group):
            ctx_ref[rows, g * HD:(g + 1) * HD] = ctx[g * BQ:(g + 1) * BQ]
    rot = kg[...]
    grad_ref[0] = (rot * cosine + rotate_back(rot * sine_t)).astype(jnp.bfloat16)
    grad_ref[1] = vg[...].astype(jnp.bfloat16)


def attend(kv_rows, queries, cotangent):
    seq = kv_rows.shape[0]
    heads = kv_rows.shape[1] // (2 * HD)
    width = queries.shape[1] // heads
    cosine, sine_t = rope_tables(seq, HD)
    return pl.pallas_call(
        attend_kernel,
        grid=(heads,),
        out_shape=(
            jax.ShapeDtypeStruct(queries.shape, jnp.bfloat16),
            jax.ShapeDtypeStruct((2, seq, heads * HD), jnp.bfloat16),
        ),
        in_specs=[
            pl.BlockSpec((seq, HD), lambda j: (0, j)),
            pl.BlockSpec((seq, HD), lambda j: (0, j + heads)),
            pl.BlockSpec((seq, width), lambda j: (0, j)),
            pl.BlockSpec((seq, width), lambda j: (0, j)),
            pl.BlockSpec((seq, HD), lambda j: (0, 0)),
            pl.BlockSpec((seq, HD), lambda j: (0, 0)),
        ],
        out_specs=(
            pl.BlockSpec((seq, width), lambda j: (0, j)),
            pl.BlockSpec((2, seq, HD), lambda j: (0, 0, j)),
        ),
        scratch_shapes=[pltpu.VMEM((seq, HD), jnp.float32), pltpu.VMEM((seq, HD), jnp.float32)],
        compiler_params=pltpu.CompilerParams(vmem_limit_bytes=VMEM_LIMIT),
        name="attend",
    )(kv_rows, kv_rows, queries, cotangent, cosine, sine_t)


def place(dims):
    dp, fs = lax.axis_index("dp"), lax.axis_index("fsdp")
    return (dp // dims[1], dp % dims[1], fs // 2), fs % 2


def target(dims, at, core, axis=None, offset=0):
    at = list(at)
    if axis is not None:
        at[axis] = (at[axis] + offset) % dims[axis]
    return (at[0] * dims[1] + at[1], at[2] * 2 + core)


def greet(peers):
    barrier = pltpu.get_barrier_semaphore()
    for peer in peers:
        pl.semaphore_signal(barrier, inc=1, device_id=peer, device_id_type=MESH)
    pl.semaphore_wait(barrier, len(peers))


def send(src, dst, send_sem, recv_sem, peer):
    return pltpu.make_async_remote_copy(
        src_ref=src, dst_ref=dst, send_sem=send_sem, recv_sem=recv_sem,
        device_id=peer, device_id_type=MESH)


ORDER = ((1, 0), (0, 1))


def reduce_kernel(dims, x1_ref, x2_ref, y1_ref, y2_ref, out_ref, *scratch):
    halves = [scratch[:11], scratch[11:]]
    at, core = place(dims)
    depth = dims[2]
    rows, cols = out_ref.shape
    half = rows // 2
    parts = y1_ref.shape[0]
    width = y1_ref.shape[2]
    peers = [target(dims, at, core, axis, k) for axis in range(3) for k in range(1, dims[axis])]
    greet(peers)

    def first_copy(h, k1, zz):
        d1 = ORDER[h][0]
        part, r1, s1, q1 = halves[h][0], halves[h][1], halves[h][5], halves[h][6]
        v1 = (at[d1] + k1) % dims[d1]
        return send(part.at[zz, v1], r1.at[k1 - 1, zz], s1.at[k1 - 1, zz], q1.at[k1 - 1, zz],
                    target(dims, at, core, d1, k1))

    def second_copy(h, k2, zz):
        d2 = ORDER[h][1]
        sum2, r2, s2, q2 = halves[h][2], halves[h][3], halves[h][7], halves[h][8]
        return send(sum2.at[k2 - 1, zz], r2.at[k2 - 1, zz], s2.at[k2 - 1, zz], q2.at[k2 - 1, zz],
                    target(dims, at, core, d2, k2))

    def third_copy(h, k):
        r3, s3, q3 = halves[h][4], halves[h][9], halves[h][10]
        part = halves[h][0]
        zz = (at[2] + k) % depth
        d1, d2 = ORDER[h]
        return send(part.at[zz, at[d1], at[d2]], r3.at[k - 1], s3.at[k - 1], q3.at[k - 1],
                    target(dims, at, core, 2, k))

    @pl.loop(1, depth + 1)
    def _(step):
        zz = (at[2] + step) % depth
        first = pl.multiple_of(zz * rows, rows)
        x1 = x1_ref[:, pl.ds(first, rows)]
        x2 = x2_ref[:, pl.ds(first, rows)]
        for part in range(parts):
            r = (mm(x1, y1_ref[part], TN) + mm(x2, y2_ref[part], TN)).astype(jnp.bfloat16)
            for i in range(width // cols):
                dp = part * (width // cols) + i
                where = (dp // dims[1], dp % dims[1])
                for h in range(2):
                    d1, d2 = ORDER[h]
                    halves[h][0][zz, where[d1], where[d2]] = (
                        r[h * half:(h + 1) * half, i * cols:(i + 1) * cols])
        for h in range(2):
            for k1 in range(1, dims[ORDER[h][0]]):
                first_copy(h, k1, zz).start()

    def keep1(h, zz, v2):
        d1, d2 = ORDER[h]
        part, r1 = halves[h][0], halves[h][1]
        total = part[zz, at[d1], v2].astype(jnp.float32)
        for k1 in range(1, dims[d1]):
            total += r1[k1 - 1, zz, v2].astype(jnp.float32)
        return total

    def second(step):
        zz = (at[2] + step) % depth
        for h in range(2):
            d1, d2 = ORDER[h]
            for k1 in range(1, dims[d1]):
                first_copy(h, k1, zz).wait_recv()
            for k2 in range(1, dims[d2]):
                v2 = (at[d2] + k2) % dims[d2]
                halves[h][2][k2 - 1, zz] = keep1(h, zz, v2).astype(jnp.bfloat16)
                second_copy(h, k2, zz).start()

    def keep2(h, zz):
        d1, d2 = ORDER[h]
        total = keep1(h, zz, at[d2])
        for k2 in range(1, dims[d2]):
            second_copy(h, k2, zz).wait_recv()
        for k2 in range(1, dims[d2]):
            total += halves[h][3][k2 - 1, zz].astype(jnp.float32)
        return total

    def third(step):
        zz = (at[2] + step) % depth
        for h in range(2):
            d1, d2 = ORDER[h]
            halves[h][0][zz, at[d1], at[d2]] = keep2(h, zz).astype(jnp.bfloat16)
            third_copy(h, step).start()

    second(1)

    @pl.loop(2, depth + 1)
    def _(step):
        second(step)
        third(step - 1)

    for h in range(2):
        total = keep2(h, at[2])
        for k in range(1, depth):
            third_copy(h, k).wait_recv()
            total += halves[h][4][k - 1].astype(jnp.float32)
        out_ref[h * half:(h + 1) * half] = total

    @pl.loop(0, depth)
    def _(zz):
        for h in range(2):
            for k1 in range(1, dims[ORDER[h][0]]):
                first_copy(h, k1, zz).wait_send()
            for k2 in range(1, dims[ORDER[h][1]]):
                second_copy(h, k2, zz).wait_send()

    @pl.loop(1, depth)
    def _(k):
        for h in range(2):
            third_copy(h, k).wait_send()


def reduce_gradient(dims, x1, x2, y1, y2, rows, cols):
    half = rows // 2
    scratch = []
    for h in range(2):
        n1, n2 = dims[ORDER[h][0]], dims[ORDER[h][1]]
        z = dims[2]
        scratch += [
            pltpu.VMEM((z, n1, n2, half, cols), jnp.bfloat16),
            pltpu.VMEM((n1 - 1, z, n2, half, cols), jnp.bfloat16),
            pltpu.VMEM((n2 - 1, z, half, cols), jnp.bfloat16),
            pltpu.VMEM((n2 - 1, z, half, cols), jnp.bfloat16),
            pltpu.VMEM((z - 1, half, cols), jnp.bfloat16),
            pltpu.SemaphoreType.DMA((n1 - 1, z)), pltpu.SemaphoreType.DMA((n1 - 1, z)),
            pltpu.SemaphoreType.DMA((n2 - 1, z)), pltpu.SemaphoreType.DMA((n2 - 1, z)),
            pltpu.SemaphoreType.DMA((z - 1,)), pltpu.SemaphoreType.DMA((z - 1,)),
        ]
    vmem = pl.BlockSpec(memory_space=pltpu.VMEM)
    return pl.pallas_call(
        functools.partial(reduce_kernel, dims),
        out_shape=jax.ShapeDtypeStruct((rows, cols), jnp.float32),
        in_specs=[vmem] * 4,
        out_specs=vmem,
        scratch_shapes=scratch,
        compiler_params=pltpu.CompilerParams(
            collective_id=1, has_side_effects=True, vmem_limit_bytes=VMEM_LIMIT),
        name="reduce_gradient",
    )(x1, x2, y1, y2)


def local(dims, hidden, queries, cotangent, point_start, point_mid, point_end, curve_time):
    t_value = curve_time[0]
    blended = (
        (1.0 - t_value) ** 2 * point_start.astype(jnp.float32)
        + 2.0 * t_value * (1.0 - t_value) * point_mid.astype(jnp.float32)
        + t_value**2 * point_end.astype(jnp.float32)
    ).astype(jnp.bfloat16)
    seq_len, model_width = hidden.shape
    rows, cols = point_mid.shape
    core = lax.axis_index("fsdp") % 2
    swap = [(i, i ^ 1) for i in range(2 * dims[2])]
    split = hidden.reshape(seq_len, dims[2], 2, rows)
    own_first = core == 0
    mine = jnp.where(own_first, split[:, :, 0], split[:, :, 1]).reshape(seq_len, -1)
    others = jnp.where(own_first, split[:, :, 1], split[:, :, 0]).reshape(seq_len, -1)
    x2 = lax.ppermute(others, "fsdp", swap)

    columns_full = lax.all_gather(blended, "dp", axis=1, tiled=True)
    full = lax.all_gather(columns_full, "fsdp", axis=0, tiled=True)
    kv_rows = jnp.dot(hidden, full, preferred_element_type=jnp.float32).astype(jnp.bfloat16)

    context, kv_grad = attend(kv_rows, queries, cotangent)
    kv_other = lax.ppermute(kv_grad, "fsdp", swap)
    gradient = reduce_gradient(dims, mine, x2, kv_grad, kv_other, rows, cols)
    return (context, gradient * (2.0 * t_value * (1.0 - t_value)))


def solution(mesh):
    dp, fsdp = mesh.shape["dp"], mesh.shape["fsdp"]
    dims = (dp // 2, 2, fsdp // 2)
    return jax.shard_map(
        functools.partial(local, dims),
        mesh=mesh,
        in_specs=(
            P(("dp", "fsdp"), None),
            P(("dp", "fsdp"), None),
            P(("dp", "fsdp"), None),
            P("fsdp", "dp"),
            P("fsdp", "dp"),
            P("fsdp", "dp"),
            P(),
        ),
        out_specs=(P(("dp", "fsdp"), None), P("fsdp", "dp")),
        check_vma=False,
    )
```

time: 430 us -> 220 us (0.51)
  waiting for transfers between devices: 266 us -> 90.9 us
  matrix products: 92.8 us -> 10.2 us
  Pallas kernels: 0 us -> 70.5 us
  local copies, waits for them, and re-layouts: 35.4 us -> 21.8 us
  other arithmetic: 16.1 us -> 8.03 us
    reduce_scatter x1 -> x0, waiting for transfers between devices: 179 us -> none  [local(): lax.psum_scatter(jnp.dot(window.T, kv_grad, preferred_element_type=jnp.fl...]
    pallas_call x0 -> x2, Pallas kernels: none -> 70.5 us  [the longest x1 54 us: reduce_gradient(): pl.pallas_call(functools.partial(reduce_kernel, dims), out_shape=jax.Shap...]
    dot_general x18 -> x1, matrix products: 72.8 us -> 10.2 us  [local(): jnp.dot(hidden, full, preferred_element_type=jnp.float32)]
    sub x4 -> x0, matrix products: 20 us -> none  [attend(): weights_exp = jnp.exp(scores - top_score)]
    unnamed x31 -> x4, local copies, waits for them, and re-layouts: 23.8 us -> 4.92 us
    reshape x4 -> x1, local copies, waits for them, and re-layouts: 1.89 us -> 7.84 us  [local(): split = hidden.reshape(seq_len, dims[2], 2, rows)]
    slice x2 -> x1, local copies, waits for them, and re-layouts: 4.07 us -> 9.06 us  [local(): split[:, :, 0]]
    transpose x1 -> x0, local copies, waits for them, and re-layouts: 4.65 us -> none  [local(): permuted = hidden.reshape(seq_len, fsdp_count, data_count, block_rows).tr...]
  transfers between devices with their start and end apart: 4 -> 4, of which waited for: 3 -> 3; matrix products, arithmetic and copies ran while one was open for 8% -> 16% of each run, Pallas kernels for 0% -> 8%
where the time goes in v1:
time: 220 us; the launch traced here: 216 us
  waiting for transfers between devices  90.9 us (41%)
  Pallas kernels  70.5 us (32%)
  local copies, waits for them, and re-layouts  21.8 us (10%)
  between operations  14.7 us (7%)
  matrix products  10.2 us (5%)
  other arithmetic  8.03 us (4%)
    all_gather x1, waiting for transfers between devices, local(): full = lax.all_gather(columns_full, 'fsdp', axis=0, tiled=True)  60.5 us
    pallas_call x1, Pallas kernels, reduce_gradient(): pl.pallas_call(functools.partial(reduce_kernel, dims), out_shape=jax.Shap...  54 us
    all_gather x1, waiting for transfers between devices, local(): columns_full = lax.all_gather(blended, 'dp', axis=1, tiled=True)  29.6 us
    pallas_call x1, Pallas kernels, attend(): pl.pallas_call(attend_kernel, grid=(heads,), out_shape=(jax.ShapeDtypeStr...  16.5 us
    dot_general x1, matrix products, local(): jnp.dot(hidden, full, preferred_element_type=jnp.float32)  10.2 us
    slice x1, local copies, waits for them, and re-layouts, local(): split[:, :, 0]  9.06 us
    reshape x1, local copies, waits for them, and re-layouts, local(): split = hidden.reshape(seq_len, dims[2], 2, rows)  7.84 us
    unnamed x4, local copies, waits for them, and re-layouts  4.92 us
  transfers between devices with their start and end apart: 4, of which 3 were waited for; matrix products, arithmetic and copies ran while one was open for 16% of the time, Pallas kernels for 8%

profile of v1, /device:TPU:0, one launch (start us, length us, event | category | flops | bytes accessed | tf_op | source)
XLA Modules:
  0.0 216.4 jit_solution(11448123864088907720)
XLA Ops:
  7.2 0.0 all-gather.3.cloned.1.call-start
  7.9 2.0 add_convert_fusion
  9.8 0.0 all-gather.3.cloned.1.call-update
  9.8 0.0 all-gather.5.cloned.1.call-start
  9.9 29.6 %all-gather.3.cloned.1.call-done = bf16[512,1024]{1,0:T(8,128)(2,1)} async-done(((bf16[512,256]{1,0:T(8,128)(2,1)}), bf16[512,1024]{1,0:T(8,128)(2,1)}) %all-gather.3.cloned.1.call-update) | async-done | bytes 1048592 | tf_op jit(solution)/shard_map/all_gather | solution.py:305
  39.5 0.0 all-gather.5.cloned.1.call-update
  39.5 7.8 %reshape.36 = bf16[512,4,2,512]{3,2,1,0:T(2,128)(2,1)} reshape(bf16[512,4096]{1,0:T(8,128)(2,1)} %param.7) | data formatting | bytes 8388608 | tf_op jit(solution)/shard_map/reshape | solution.py:299
  47.4 9.1 %fusion.3 = (bf16[512,4,1,512]{3,2,1,0:T(2,128)(2,1)S(1)}, bf16[512,4,1,512]{3,2,1,0:T(2,128)(2,1)S(1)}) fusion(bf16[512,4,2,512]{3,2,1,0:T(2,128)(2,1)} %reshape.36), kind=kLoop, calls=%fused_computation.12 | loop fusion | bytes 8388608 | tf_op jit(solution)/shard_map/slice | solution.py:301
  56.4 2.2 %broadcast_select_fusion = (bf16[512,4,1,512]{3,1,0,2:T(4,128)(2,1)S(1)}, bf16[512,4,1,512]{3,1,0,2:T(4,128)(2,1)S(1)}) fusion(pred[]{:T(512)S(6)} %eq.5, bf16[512,4,1,512]{3,2,1,0:T(2,128)(2,1)S(1)} %get-tuple-element.9, bf16[512,4,1,512]{3,2,1,0:T(2,128)(2,1)S(1)} %get-tuple-element.8), kind=kLoop, calls=%fused_computation | loop fusion | flops 2097152 | bytes 8388609 | tf_op jit(solution)/shard_map/jit(_where)/select_n | solution.py:302
  58.7 2.0 copy.16
  60.6 0.0 collective-permute-start
  60.6 1.0 fusion.1
  61.6 1.0 pad_maximum_fusion
  62.6 60.5 %all-gather.5.cloned.1.call-done = bf16[4096,1024]{1,0:T(8,128)(2,1)} async-done(((bf16[512,1024]{1,0:T(8,128)(2,1)}), bf16[4096,1024]{1,0:T(8,128)(2,1)}) %all-gather.5.cloned.1.call-update) | async-done | bytes 8388624 | tf_op jit(solution)/shard_map/all_gather | solution.py:306
  123.2 10.2 %fusion.k_ref.v_ref = bf16[512,1024]{1,0:T(8,128)(2,1)} fusion(bf16[512,4096]{1,0:T(8,128)(2,1)} %param.7, bf16[4096,1024]{1,0:T(8,128)(2,1)} %all-gather.5.cloned.1.call-done), kind=kOutput, calls=%fused_computation.3 | convolution fusion | flops 4295491584 | bytes 13631488 | tf_op jit(solution)/shard_map/dot_general | solution.py:307
  133.4 16.5 %attend.1 = (bf16[512,2048]{1,0:T(8,128)(2,1)}, bf16[2,512,512]{2,1,0:T(8,128)(2,1)}) custom-call(bf16[512,1024]{1,0:T(8,128)(2,1)} %fusion.k_ref.v_ref, bf16[512,1024]{1,0:T(8,128)(2,1)} %fusion.k_ref.v_ref, bf16[512,2048]{1,0:T(8,128)(2,1)} %q_ref.1, bf16[512,2048]{1,0:T(8,128)(2,1)} %g_ref.1, f32[512,128]{1,0:T(8,128)} %get-tuple-element.12.cos_ref, ...), custom_call_target="tpu_custom_call" | custom-call | tf_op jit(solution)/shard_map/attend/pallas_call | solution.py:92
  149.9 0.2 collective-permute-start.1
  150.1 2.0 copy.15
  152.0 0.0 collective-permute-done.x2_ref
  152.0 0.7 collective-permute-done.1.y2_ref
  152.7 0.0 copy-start
  152.7 1.0 copy-done
  153.7 54.0 %reduce_gradient.1 = f32[512,256]{1,0:T(8,128)} custom-call(bf16[512,2048]{1,0:T(8,128)(2,1)} %bitcast.17, bf16[512,2048]{1,0:T(8,128)(2,1)} %collective-permute-done.x2_ref, bf16[2,512,512]{2,1,0:T(8,128)(2,1)} %get-tuple-element.5.y1_ref, bf16[2,512,512]{2,1,0:T(8,128)(2,1)} %copy-done), custom_call_target="tpu_custom_call" | custom-call | tf_op jit(solution)/shard_map/reduce_gradient/pallas_call | solution.py:276
  207.7 1.9 broadcast_multiply_fusion
  (1 shorter events, 0.0 us)
Async XLA Ops:
  7.2 32.3 %all-gather.3.cloned.1.call-start = ((), (), s32[]{:S(2)}) async-start(), calls=%async_computation | async-start | bytes 1310720 | tf_op jit(solution)/shard_map/all_gather | solution.py:305
  9.8 113.3 %all-gather.5.cloned.1.call-start = ((), (), s32[]{:S(2)}) async-start(), calls=%async_computation.1 | async-start | bytes 9437184 | tf_op jit(solution)/shard_map/all_gather | solution.py:306
  60.6 91.4 %collective-permute-start = (bf16[512,2048]{1,0:T(8,128)(2,1)}, bf16[512,2048]{1,0:T(8,128)(2,1)}, u32[]{:S(2)}, u32[]{:S(2)}) collective-permute-start(bf16[512,2048]{1,0:T(8,128)(2,1)} %bitcast.11), channel_id=1, source_target_pairs={{0,1},{1,0},{2,3},{3,2},{4,5},{5,4},{6,7},{7,6},{8,9},{9,8},{10,11... | collective-permute-start | bytes 6291464 | tf_op jit(solution)/shard_map/ppermute | solution.py:303
  149.9 2.9 %collective-permute-start.1 = (bf16[2,512,512]{2,1,0:T(8,128)(2,1)}, bf16[2,512,512]{2,1,0:T(8,128)(2,1)S(1)}, u32[]{:S(2)}, u32[]{:S(2)}) collective-permute-start(bf16[2,512,512]{2,1,0:T(8,128)(2,1)} %get-tuple-element.5.y1_ref), channel_id=1, source_target_pairs={{0,1},{1,0},{2,3},{3,2},{4,5},{5,4},{6,7},{7,6},{8,9},{9,8},{10,11... | collective-permute-start | bytes 3145736 | tf_op jit(solution)/shard_map/ppermute | solution.py:310
  152.7 1.0 copy-start
Sparse Core Ops, SparseCore 0:
  10.4 29.0 all-gather.2
  41.1 82.0 all-gather.4

commit v2 on v1

--- a/solution.py
+++ b/solution.py
@@ -114,6 +114,9 @@
     )(kv_rows, kv_rows, queries, cotangent, cosine, sine_t)
 
 
+ORDER = ((1, 0), (0, 1))
+
+
 def place(dims):
     dp, fs = lax.axis_index("dp"), lax.axis_index("fsdp")
     return (dp // dims[1], dp % dims[1], fs // 2), fs % 2
@@ -139,10 +142,207 @@
         device_id=peer, device_id_type=MESH)
 
 
-ORDER = ((1, 0), (0, 1))
-
-
-def reduce_kernel(dims, x1_ref, x2_ref, y1_ref, y2_ref, out_ref, *scratch):
+def all_peers(dims, at, core):
+    peers = [target(dims, at, core, axis, k) for axis in range(3) for k in range(1, dims[axis])]
+    return peers + [target(dims, at, 1 - core)]
+
+
+def gather_kernel(dims, block_ref, hidden_ref, kv_ref, x2_ref, full, acc, load_sem, x_send, x_recv,
+                  recv, z_send, s2, s3, c_send):
+    at, core = place(dims)
+    depth = dims[2]
+    rows, cols = block_ref.shape
+    half = rows // 2
+    other = target(dims, at, 1 - core)
+
+    def piece(c, h, zz, pos):
+        return full.at[c, zz, pos[0], pos[1], pl.ds(h * half, half)]
+
+    def cell(h, zz, pos):
+        return recv.at[core, h, zz, pos[0], pos[1]]
+
+    def moved(axis, k):
+        pos = [at[0], at[1]]
+        pos[axis] = (pos[axis] + k) % dims[axis]
+        return pos
+
+    def push(h, zz, pos, send_sem, peer):
+        ref = piece(core, h, zz, pos)
+        return send(ref, ref, send_sem, cell(h, zz, pos), peer)
+
+    def to_z(h, k):
+        return push(h, at[2], at[:2], z_send.at[h, k - 1], target(dims, at, core, 2, k))
+
+    def to_second(h, zz, k):
+        d2 = ORDER[1 - h][0]
+        return push(h, zz, at[:2], s2[h].at[k - 1, zz], target(dims, at, core, d2, k))
+
+    def to_third(h, zz, pos, k):
+        d2, d3 = ORDER[1 - h]
+        return push(h, zz, pos, s3[h].at[k - 1, zz, pos[d2]], target(dims, at, core, d3, k))
+
+    def to_core(h, zz, pos):
+        ref = piece(core, h, zz, pos)
+        return send(ref, ref, c_send.at[h, zz, pos[0], pos[1]], cell(h, zz, pos), other)
+
+    def swap(zz):
+        src = pl.multiple_of((2 * zz + 1 - core) * rows, rows)
+        dst = pl.multiple_of(zz * rows, rows)
+        return send(hidden_ref.at[:, pl.ds(src, rows)], x2_ref.at[:, pl.ds(dst, rows)],
+                    x_send.at[zz], x_recv.at[zz], other)
+
+    def arrived(c, h, zz, pos):
+        ref = piece(c, h, zz, pos)
+        send(ref, ref, c_send.at[h, zz, pos[0], pos[1]], recv.at[c, h, zz, pos[0], pos[1]],
+             other).wait_recv()
+
+    def relay_first(h, zz):
+        d2, d3 = ORDER[1 - h]
+        for k in range(1, dims[d2]):
+            to_second(h, zz, k).start()
+        for k in range(1, dims[d3]):
+            to_third(h, zz, at[:2], k).start()
+        to_core(h, zz, at[:2]).start()
+
+    def relay_second(zz):
+        for h in range(2):
+            d2, d3 = ORDER[1 - h]
+            for k2 in range(1, dims[d2]):
+                pos = moved(d2, k2)
+                arrived(core, h, zz, pos)
+                for k in range(1, dims[d3]):
+                    to_third(h, zz, pos, k).start()
+                to_core(h, zz, pos).start()
+
+    def product(c, zz, first):
+        x = hidden_ref[:, pl.ds(pl.multiple_of((2 * zz + c) * rows, rows), rows)]
+        for dp in range(dims[0] * dims[1]):
+            w = full[c, zz, dp // dims[1], dp % dims[1]]
+            got = mm(x, w)
+            if first:
+                acc[:, dp * cols:(dp + 1) * cols] = got
+            else:
+                acc[:, dp * cols:(dp + 1) * cols] += got
+
+    def relay_third(zz):
+        for h in range(2):
+            d2, d3 = ORDER[1 - h]
+            for k3 in range(1, dims[d3]):
+                for k2 in range(dims[d2]):
+                    pos = moved(d3, k3)
+                    pos[d2] = (at[d2] + k2) % dims[d2]
+                    arrived(core, h, zz, pos)
+                    to_core(h, zz, pos).start()
+
+    def from_core(zz):
+        for h in range(2):
+            for i in range(dims[0]):
+                for j in range(dims[1]):
+                    arrived(1 - core, h, zz, (i, j))
+
+    loads = [pltpu.make_async_copy(block_ref.at[pl.ds(h * half, half)], piece(core, h, at[2], at[:2]),
+                                   load_sem.at[h]) for h in range(2)]
+    for load in loads:
+        load.start()
+    greet(all_peers(dims, at, core))
+    for load in loads:
+        load.wait()
+    for h in range(2):
+        for k in range(1, depth):
+            to_z(h, k).start()
+        relay_first(h, at[2])
+
+    @pl.loop(1, depth)
+    def _(k):
+        zz = (at[2] + depth - k) % depth
+        for h in range(2):
+            arrived(core, h, zz, at[:2])
+            relay_first(h, zz)
+        relay_second((zz + 1) % depth)
+
+    relay_second((at[2] + 1) % depth)
+
+    @pl.loop(0, depth)
+    def _(zz):
+        swap(zz).start()
+
+    relay_third(at[2])
+    product(core, at[2], True)
+
+    @pl.loop(1, depth)
+    def _(k):
+        zz = (at[2] + depth - k) % depth
+        before = (zz + 1) % depth
+        relay_third(zz)
+        product(core, zz, False)
+        from_core(before)
+        product(1 - core, before, False)
+
+    last = (at[2] + 1) % depth
+    from_core(last)
+    product(1 - core, last, False)
+    kv_ref[...] = acc[...].astype(jnp.bfloat16)
+
+    for h in range(2):
+        for k in range(1, depth):
+            to_z(h, k).wait_send()
+
+    @pl.loop(0, depth)
+    def _(zz):
+        swap(zz).wait()
+        for h in range(2):
+            d2, d3 = ORDER[1 - h]
+            for k in range(1, dims[d2]):
+                to_second(h, zz, k).wait_send()
+            for k in range(1, dims[d3]):
+                for k2 in range(dims[d2]):
+                    pos = moved(d2, k2)
+                    to_third(h, zz, pos, k).wait_send()
+            for i in range(dims[0]):
+                for j in range(dims[1]):
+                    to_core(h, zz, (i, j)).wait_send()
+
+
+def gather_project(dims, blended, hidden):
+    rows, cols = blended.shape
+    seq = hidden.shape[0]
+    a, b, z = dims
+    width = a * b * cols
+    sem = pltpu.SemaphoreType.DMA
+
+    def body(*refs):
+        gather_kernel(dims, *refs[:10], refs[10], (refs[11], refs[12]), (refs[13], refs[14]), refs[15])
+
+    def sems(h):
+        d2, d3 = ORDER[1 - h]
+        return dims[d2], dims[d3]
+
+    vmem = pl.BlockSpec(memory_space=pltpu.VMEM)
+    return pl.pallas_call(
+        body,
+        out_shape=(
+            jax.ShapeDtypeStruct((seq, width), jnp.bfloat16),
+            jax.ShapeDtypeStruct((seq, z * rows), jnp.bfloat16),
+        ),
+        in_specs=[pl.BlockSpec(memory_space=pl.ANY), vmem],
+        out_specs=(vmem, pl.BlockSpec(memory_space=pl.ANY)),
+        scratch_shapes=[
+            pltpu.VMEM((2, z, a, b, rows, cols), jnp.bfloat16),
+            pltpu.VMEM((seq, width), jnp.float32),
+            sem((2,)), sem((z,)), sem((z,)),
+            sem((2, 2, z, a, b)),
+            sem((2, z - 1)),
+            *[sem((sems(h)[0] - 1, z)) for h in range(2)],
+            *[sem((sems(h)[1] - 1, z, sems(h)[0])) for h in range(2)],
+            sem((2, z, a, b)),
+        ],
+        compiler_params=pltpu.CompilerParams(
+            collective_id=2, has_side_effects=True, vmem_limit_bytes=VMEM_LIMIT),
+        name="gather_project",
+    )(blended, hidden)
+
+
+def reduce_kernel(dims, x1_ref, x2_ref, y1_ref, out_ref, y2_ref, swap_send, swap_recv, *scratch):
     halves = [scratch[:11], scratch[11:]]
     at, core = place(dims)
     depth = dims[2]
@@ -150,8 +350,11 @@
     half = rows // 2
     parts = y1_ref.shape[0]
     width = y1_ref.shape[2]
-    peers = [target(dims, at, core, axis, k) for axis in range(3) for k in range(1, dims[axis])]
-    greet(peers)
+    other = target(dims, at, 1 - core)
+    greet(all_peers(dims, at, core))
+    swap = send(y1_ref, y2_ref, swap_send, swap_recv, other)
+    swap.start()
+    swap.wait()
 
     def first_copy(h, k1, zz):
         d1 = ORDER[h][0]
@@ -177,9 +380,8 @@
     @pl.loop(1, depth + 1)
     def _(step):
         zz = (at[2] + step) % depth
-        first = pl.multiple_of(zz * rows, rows)
-        x1 = x1_ref[:, pl.ds(first, rows)]
-        x2 = x2_ref[:, pl.ds(first, rows)]
+        x1 = x1_ref[:, pl.ds(pl.multiple_of((2 * zz + core) * rows, rows), rows)]
+        x2 = x2_ref[:, pl.ds(pl.multiple_of(zz * rows, rows), rows)]
         for part in range(parts):
             r = (mm(x1, y1_ref[part], TN) + mm(x2, y2_ref[part], TN)).astype(jnp.bfloat16)
             for i in range(width // cols):
@@ -256,9 +458,9 @@
             third_copy(h, k).wait_send()
 
 
-def reduce_gradient(dims, x1, x2, y1, y2, rows, cols):
+def reduce_gradient(dims, x1, x2, y1, rows, cols):
     half = rows // 2
-    scratch = []
+    scratch = [pltpu.VMEM(y1.shape, y1.dtype), pltpu.SemaphoreType.DMA, pltpu.SemaphoreType.DMA]
     for h in range(2):
         n1, n2 = dims[ORDER[h][0]], dims[ORDER[h][1]]
         z = dims[2]
@@ -276,13 +478,13 @@
     return pl.pallas_call(
         functools.partial(reduce_kernel, dims),
         out_shape=jax.ShapeDtypeStruct((rows, cols), jnp.float32),
-        in_specs=[vmem] * 4,
+        in_specs=[vmem] * 3,
         out_specs=vmem,
         scratch_shapes=scratch,
         compiler_params=pltpu.CompilerParams(
             collective_id=1, has_side_effects=True, vmem_limit_bytes=VMEM_LIMIT),
         name="reduce_gradient",
-    )(x1, x2, y1, y2)
+    )(x1, x2, y1)
 
 
 def local(dims, hidden, queries, cotangent, point_start, point_mid, point_end, curve_time):
@@ -292,23 +494,10 @@
         + 2.0 * t_value * (1.0 - t_value) * point_mid.astype(jnp.float32)
         + t_value**2 * point_end.astype(jnp.float32)
     ).astype(jnp.bfloat16)
-    seq_len, model_width = hidden.shape
     rows, cols = point_mid.shape
-    core = lax.axis_index("fsdp") % 2
-    swap = [(i, i ^ 1) for i in range(2 * dims[2])]
-    split = hidden.reshape(seq_len, dims[2], 2, rows)
-    own_first = core == 0
-    mine = jnp.where(own_first, split[:, :, 0], split[:, :, 1]).reshape(seq_len, -1)
-    others = jnp.where(own_first, split[:, :, 1], split[:, :, 0]).reshape(seq_len, -1)
-    x2 = lax.ppermute(others, "fsdp", swap)
-
-    columns_full = lax.all_gather(blended, "dp", axis=1, tiled=True)
-    full = lax.all_gather(columns_full, "fsdp", axis=0, tiled=True)
-    kv_rows = jnp.dot(hidden, full, preferred_element_type=jnp.float32).astype(jnp.bfloat16)
-
+    kv_rows, x2 = gather_project(dims, blended, hidden)
     context, kv_grad = attend(kv_rows, queries, cotangent)
-    kv_other = lax.ppermute(kv_grad, "fsdp", swap)
-    gradient = reduce_gradient(dims, mine, x2, kv_grad, kv_other, rows, cols)
+    gradient = reduce_gradient(dims, hidden, x2, kv_grad, rows, cols)
     return (context, gradient * (2.0 * t_value * (1.0 - t_value)))
 
 

time: 220 us -> 147 us (0.67)
  the two profiles are of different devices: /device:TPU:0 before, /device:TPU:9 now
where the time goes in v2:
time: 147 us
  Pallas kernels  140 us (95%)
  other arithmetic  5.83 us (4%)
    pallas_call x1, Pallas kernels, reduce_gradient(): pl.pallas_call(functools.partial(reduce_kernel, dims), out_shape=jax.Shap...  69.6 us
    pallas_call x1, Pallas kernels, gather_project(): pl.pallas_call(body, out_shape=(jax.ShapeDtypeStruct((seq, width), jnp.bf...  53.5 us
    pallas_call x1, Pallas kernels, attend(): pl.pallas_call(attend_kernel, grid=(heads,), out_shape=(jax.ShapeDtypeStr...  16.5 us

profile of v2, /device:TPU:9, one launch (start us, length us, event | category | flops | bytes accessed | tf_op | source)
XLA Modules:
  0.0 146.8 jit_solution(5596663015567614294)
XLA Ops:
  1.3 2.0 %add_convert_fusion.refs_0_ = bf16[512,256]{1,0:T(8,128)(2,1)} fusion(bf16[512,256]{1,0:T(8,128)(2,1)} %param.12, bf16[512,256]{1,0:T(8,128)(2,1)} %param.11, bf16[512,256]{1,0:T(8,128)(2,1)} %param.10, f32[]{:T(128)} %bitcast.2, f32[]{:T(128)} %bitcast.1, f32[]{:T(128)} %bitcast), kind=kLoop, calls=%fused_computation | loop fusion | flops 1179648 | bytes 1048588 | tf_op jit(solution)/shard_map/convert_element_type | solution.py:496
  3.3 1.0 fusion
  4.2 1.0 pad_maximum_fusion
  5.2 53.5 %gather_project.1 = (bf16[512,1024]{1,0:T(8,128)(2,1)}, bf16[512,2048]{1,0:T(8,128)(2,1)}) custom-call(bf16[512,256]{1,0:T(8,128)(2,1)} %add_convert_fusion.refs_0_, bf16[512,4096]{1,0:T(8,128)(2,1)} %x1_ref.1), custom_call_target="tpu_custom_call" | custom-call | tf_op jit(solution)/shard_map/gather_project/pallas_call | solution.py:321
  58.8 16.5 %attend.1 = (bf16[512,2048]{1,0:T(8,128)(2,1)}, bf16[2,512,512]{2,1,0:T(8,128)(2,1)}) custom-call(bf16[512,1024]{1,0:T(8,128)(2,1)} %get-tuple-element.6.k_ref.v_ref, bf16[512,1024]{1,0:T(8,128)(2,1)} %get-tuple-element.6.k_ref.v_ref, bf16[512,2048]{1,0:T(8,128)(2,1)} %q_ref.1, bf16[512,2048]{1,0:T(8,128)(2,1)} %g_ref.1, ...), custom_call_target="tpu_custom_call" | custom-call | tf_op jit(solution)/shard_map/attend/pallas_call | solution.py:92
  75.3 69.6 %reduce_gradient.1 = f32[512,256]{1,0:T(8,128)} custom-call(bf16[512,4096]{1,0:T(8,128)(2,1)} %x1_ref.1, bf16[512,2048]{1,0:T(8,128)(2,1)} %get-tuple-element.8.x2_ref, bf16[2,512,512]{2,1,0:T(8,128)(2,1)} %get-tuple-element.9.y1_ref), custom_call_target="tpu_custom_call" | custom-call | tf_op jit(solution)/shard_map/reduce_gradient/pallas_call | solution.py:478
  144.9 1.9 %broadcast_multiply_fusion = f32[512,256]{1,0:T(8,128)} fusion(f32[512,256]{1,0:T(8,128)} %reduce_gradient.1, f32[]{:T(128)} %bitcast.1), kind=kLoop, calls=%fused_computation.6 | loop fusion | flops 131072 | bytes 1048580 | tf_op jit(solution)/shard_map/mul | solution.py:501
  (1 shorter events, 0.0 us)

commit v3 on v2

--- a/solution.py
+++ b/solution.py
@@ -170,8 +170,18 @@
         ref = piece(core, h, zz, pos)
         return send(ref, ref, send_sem, cell(h, zz, pos), peer)
 
-    def to_z(h, k):
-        return push(h, at[2], at[:2], z_send.at[h, k - 1], target(dims, at, core, 2, k))
+    def to_z(h, zz, side):
+        return push(h, zz, at[:2], z_send.at[h, side, zz],
+                    target(dims, at, core, 2, (1, dims[2] - 1)[side]))
+
+    def sides(act):
+        pl.when(at[2] < depth - 1)(lambda: act(0))
+        pl.when(at[2] > 0)(lambda: act(1))
+
+    def near(k, act):
+        below, above = at[2] - k, at[2] + k
+        pl.when(below >= 0)(lambda: act(below, 0))
+        pl.when(above < depth)(lambda: act(above, 1))
 
     def to_second(h, zz, k):
         d2 = ORDER[1 - h][0]
@@ -247,20 +257,31 @@
     greet(all_peers(dims, at, core))
     for load in loads:
         load.wait()
+    def start_z(zz, side):
+        for h in range(2):
+            to_z(h, zz, side).start()
+
+    sides(lambda side: start_z(at[2], side))
     for h in range(2):
-        for k in range(1, depth):
-            to_z(h, k).start()
         relay_first(h, at[2])
 
-    @pl.loop(1, depth)
+    def take_z(zz, side):
+        for h in range(2):
+            arrived(core, h, zz, at[:2])
+        more = at[2] < depth - 1 if side == 0 else at[2] > 0
+        pl.when(more)(lambda: start_z(zz, side))
+        for h in range(2):
+            relay_first(h, zz)
+
+    near(1, take_z)
+    relay_second(at[2])
+
+    @pl.loop(2, depth)
     def _(k):
-        zz = (at[2] + depth - k) % depth
-        for h in range(2):
-            arrived(core, h, zz, at[:2])
-            relay_first(h, zz)
-        relay_second((zz + 1) % depth)
-
-    relay_second((at[2] + 1) % depth)
+        near(k, take_z)
+        near(k - 1, lambda zz, side: relay_second(zz))
+
+    near(depth - 1, lambda zz, side: relay_second(zz))
 
     @pl.loop(0, depth)
     def _(zz):
@@ -269,23 +290,30 @@
     relay_third(at[2])
     product(core, at[2], True)
 
-    @pl.loop(1, depth)
-    def _(k):
-        zz = (at[2] + depth - k) % depth
-        before = (zz + 1) % depth
+    def finish_core(zz):
+        from_core(zz)
+        product(1 - core, zz, False)
+
+    def third_near(zz, side):
         relay_third(zz)
         product(core, zz, False)
-        from_core(before)
-        product(1 - core, before, False)
-
-    last = (at[2] + 1) % depth
-    from_core(last)
-    product(1 - core, last, False)
+
+    near(1, third_near)
+    finish_core(at[2])
+
+    @pl.loop(2, depth)
+    def _(k):
+        near(k, third_near)
+        near(k - 1, lambda zz, side: finish_core(zz))
+
+    near(depth - 1, lambda zz, side: finish_core(zz))
     kv_ref[...] = acc[...].astype(jnp.bfloat16)
 
-    for h in range(2):
-        for k in range(1, depth):
-            to_z(h, k).wait_send()
+    @pl.loop(0, depth)
+    def _(zz):
+        for h in range(2):
+            pl.when((zz <= at[2]) & (at[2] < depth - 1))(lambda: to_z(h, zz, 0).wait_send())
+            pl.when((zz >= at[2]) & (at[2] > 0))(lambda: to_z(h, zz, 1).wait_send())
 
     @pl.loop(0, depth)
     def _(zz):
@@ -331,7 +359,7 @@
             pltpu.VMEM((seq, width), jnp.float32),
             sem((2,)), sem((z,)), sem((z,)),
             sem((2, 2, z, a, b)),
-            sem((2, z - 1)),
+            sem((2, 2, z)),
             *[sem((sems(h)[0] - 1, z)) for h in range(2)],
             *[sem((sems(h)[1] - 1, z, sems(h)[0])) for h in range(2)],
             sem((2, z, a, b)),
@@ -377,8 +405,7 @@
         return send(part.at[zz, at[d1], at[d2]], r3.at[k - 1], s3.at[k - 1], q3.at[k - 1],
                     target(dims, at, core, 2, k))
 
-    @pl.loop(1, depth + 1)
-    def _(step):
+    def compute(step):
         zz = (at[2] + step) % depth
         x1 = x1_ref[:, pl.ds(pl.multiple_of((2 * zz + core) * rows, rows), rows)]
         x2 = x2_ref[:, pl.ds(pl.multiple_of(zz * rows, rows), rows)]
@@ -430,12 +457,20 @@
             halves[h][0][zz, at[d1], at[d2]] = keep2(h, zz).astype(jnp.bfloat16)
             third_copy(h, step).start()
 
+    @pl.loop(1, 3)
+    def _(step):
+        compute(step)
+
     second(1)
 
-    @pl.loop(2, depth + 1)
+    @pl.loop(3, depth + 1)
     def _(step):
-        second(step)
-        third(step - 1)
+        compute(step)
+        second(step - 1)
+        third(step - 2)
+
+    second(depth)
+    third(depth - 1)
 
     for h in range(2):
         total = keep2(h, at[2])

time: 147 us -> 129 us (0.88)
  the two profiles are of different devices: /device:TPU:9 before, /device:TPU:0 now
where the time goes in v3:
time: 129 us
  Pallas kernels  122 us (95%)
  other arithmetic  5.83 us (5%)
  between operations  1.3 us (1%)
    pallas_call x1, Pallas kernels, reduce_gradient(): pl.pallas_call(functools.partial(reduce_kernel, dims), out_shape=jax.Shap...  53.6 us
    pallas_call x1, Pallas kernels, gather_project(): pl.pallas_call(body, out_shape=(jax.ShapeDtypeStruct((seq, width), jnp.bf...  51.6 us
    pallas_call x1, Pallas kernels, attend(): pl.pallas_call(attend_kernel, grid=(heads,), out_shape=(jax.ShapeDtypeStr...  16.5 us

profile of v3, /device:TPU:0, one launch (start us, length us, event | category | flops | bytes accessed | tf_op | source)
XLA Modules:
  0.0 128.8 jit_solution(7888358596038253363)
XLA Ops:
  1.3 2.0 %add_convert_fusion.refs_0_ = bf16[512,256]{1,0:T(8,128)(2,1)} fusion(bf16[512,256]{1,0:T(8,128)(2,1)} %param.12, bf16[512,256]{1,0:T(8,128)(2,1)} %param.11, bf16[512,256]{1,0:T(8,128)(2,1)} %param.10, f32[]{:T(128)} %bitcast.2, f32[]{:T(128)} %bitcast.1, f32[]{:T(128)} %bitcast), kind=kLoop, calls=%fused_computation | loop fusion | flops 1179648 | bytes 1048588 | tf_op jit(solution)/shard_map/convert_element_type | solution.py:531
  3.3 1.0 fusion
  4.2 1.0 pad_maximum_fusion
  5.2 51.6 %gather_project.1 = (bf16[512,1024]{1,0:T(8,128)(2,1)}, bf16[512,2048]{1,0:T(8,128)(2,1)}) custom-call(bf16[512,256]{1,0:T(8,128)(2,1)} %add_convert_fusion.refs_0_, bf16[512,4096]{1,0:T(8,128)(2,1)} %x1_ref.1), custom_call_target="tpu_custom_call" | custom-call | tf_op jit(solution)/shard_map/gather_project/pallas_call | solution.py:349
  56.8 16.5 %attend.1 = (bf16[512,2048]{1,0:T(8,128)(2,1)}, bf16[2,512,512]{2,1,0:T(8,128)(2,1)}) custom-call(bf16[512,1024]{1,0:T(8,128)(2,1)} %get-tuple-element.6.k_ref.v_ref, bf16[512,1024]{1,0:T(8,128)(2,1)} %get-tuple-element.6.k_ref.v_ref, bf16[512,2048]{1,0:T(8,128)(2,1)} %q_ref.1, bf16[512,2048]{1,0:T(8,128)(2,1)} %g_ref.1, ...), custom_call_target="tpu_custom_call" | custom-call | tf_op jit(solution)/shard_map/attend/pallas_call | solution.py:92
  73.4 53.6 %reduce_gradient.1 = f32[512,256]{1,0:T(8,128)} custom-call(bf16[512,4096]{1,0:T(8,128)(2,1)} %x1_ref.1, bf16[512,2048]{1,0:T(8,128)(2,1)} %get-tuple-element.8.x2_ref, bf16[2,512,512]{2,1,0:T(8,128)(2,1)} %get-tuple-element.9.y1_ref), custom_call_target="tpu_custom_call" | custom-call | tf_op jit(solution)/shard_map/reduce_gradient/pallas_call | solution.py:513
  127.0 1.9 %broadcast_multiply_fusion = f32[512,256]{1,0:T(8,128)} fusion(f32[512,256]{1,0:T(8,128)} %reduce_gradient.1, f32[]{:T(128)} %bitcast.1), kind=kLoop, calls=%fused_computation.6 | loop fusion | flops 131072 | bytes 1048580 | tf_op jit(solution)/shard_map/mul | solution.py:536
  (1 shorter events, 0.0 us)

commit v4 on v3

--- a/solution.py
+++ b/solution.py
@@ -16,12 +16,13 @@
 
 
 def rope_tables(seq_len, head_dim):
-    positions = jnp.arange(seq_len, dtype=jnp.float32)[:, None]
-    halves_index = jnp.arange(head_dim // 2, dtype=jnp.float32)[None, :]
+    shape = (seq_len, head_dim)
+    positions = lax.broadcasted_iota(jnp.int32, shape, 0).astype(jnp.float32)
+    column = lax.broadcasted_iota(jnp.int32, shape, 1)
+    halves_index = jnp.where(column < head_dim // 2, column, column - head_dim // 2).astype(jnp.float32)
     inverse = jnp.exp(-(2.0 * halves_index / head_dim) * math.log(500000.0))
     angles = positions * inverse
-    cosine = jnp.concatenate([jnp.cos(angles), jnp.cos(angles)], axis=1)
-    sine_t = jnp.concatenate([jnp.sin(angles), jnp.sin(angles)], axis=1)
+    cosine, sine_t = jnp.cos(angles), jnp.sin(angles)
     return (cosine, sine_t)
 
 
@@ -84,11 +85,10 @@
     grad_ref[1] = vg[...].astype(jnp.bfloat16)
 
 
-def attend(kv_rows, queries, cotangent):
+def attend(kv_rows, queries, cotangent, cosine, sine_t):
     seq = kv_rows.shape[0]
     heads = kv_rows.shape[1] // (2 * HD)
     width = queries.shape[1] // heads
-    cosine, sine_t = rope_tables(seq, HD)
     return pl.pallas_call(
         attend_kernel,
         grid=(heads,),
@@ -147,7 +147,7 @@
     return peers + [target(dims, at, 1 - core)]
 
 
-def gather_kernel(dims, block_ref, hidden_ref, kv_ref, x2_ref, full, acc, load_sem, x_send, x_recv,
+def gather_kernel(dims, block_ref, hidden_ref, kv_ref, x2_ref, cos_ref, sin_ref, full, acc, hid, load_sem, x_send, x_recv,
                   recv, z_send, s2, s3, c_send):
     at, core = place(dims)
     depth = dims[2]
@@ -225,7 +225,7 @@
                 to_core(h, zz, pos).start()
 
     def product(c, zz, first):
-        x = hidden_ref[:, pl.ds(pl.multiple_of((2 * zz + c) * rows, rows), rows)]
+        x = hid[:, pl.ds(pl.multiple_of((2 * zz + c) * rows, rows), rows)]
         for dp in range(dims[0] * dims[1]):
             w = full[c, zz, dp // dims[1], dp % dims[1]]
             got = mm(x, w)
@@ -254,6 +254,8 @@
                                    load_sem.at[h]) for h in range(2)]
     for load in loads:
         load.start()
+    whole = pltpu.make_async_copy(hidden_ref, hid, load_sem.at[2])
+    whole.start()
     greet(all_peers(dims, at, core))
     for load in loads:
         load.wait()
@@ -265,6 +267,14 @@
     for h in range(2):
         relay_first(h, at[2])
 
+    @pl.loop(0, depth)
+    def _(zz):
+        swap(zz).start()
+
+    cosine, sine_t = rope_tables(*cos_ref.shape)
+    cos_ref[...] = cosine
+    sin_ref[...] = sine_t
+
     def take_z(zz, side):
         for h in range(2):
             arrived(core, h, zz, at[:2])
@@ -283,10 +293,7 @@
 
     near(depth - 1, lambda zz, side: relay_second(zz))
 
-    @pl.loop(0, depth)
-    def _(zz):
-        swap(zz).start()
-
+    whole.wait()
     relay_third(at[2])
     product(core, at[2], True)
 
@@ -339,7 +346,7 @@
     sem = pltpu.SemaphoreType.DMA
 
     def body(*refs):
-        gather_kernel(dims, *refs[:10], refs[10], (refs[11], refs[12]), (refs[13], refs[14]), refs[15])
+        gather_kernel(dims, *refs[:14], (refs[14], refs[15]), (refs[16], refs[17]), refs[18])
 
     def sems(h):
         d2, d3 = ORDER[1 - h]
@@ -351,13 +358,16 @@
         out_shape=(
             jax.ShapeDtypeStruct((seq, width), jnp.bfloat16),
             jax.ShapeDtypeStruct((seq, z * rows), jnp.bfloat16),
+            jax.ShapeDtypeStruct((seq, HD), jnp.float32),
+            jax.ShapeDtypeStruct((seq, HD), jnp.float32),
         ),
-        in_specs=[pl.BlockSpec(memory_space=pl.ANY), vmem],
-        out_specs=(vmem, pl.BlockSpec(memory_space=pl.ANY)),
+        in_specs=[pl.BlockSpec(memory_space=pl.ANY)] * 2,
+        out_specs=(vmem, pl.BlockSpec(memory_space=pl.ANY), vmem, vmem),
         scratch_shapes=[
             pltpu.VMEM((2, z, a, b, rows, cols), jnp.bfloat16),
             pltpu.VMEM((seq, width), jnp.float32),
-            sem((2,)), sem((z,)), sem((z,)),
+            pltpu.VMEM(hidden.shape, hidden.dtype),
+            sem((3,)), sem((z,)), sem((z,)),
             sem((2, 2, z, a, b)),
             sem((2, 2, z)),
             *[sem((sems(h)[0] - 1, z)) for h in range(2)],
@@ -370,7 +380,8 @@
     )(blended, hidden)
 
 
-def reduce_kernel(dims, x1_ref, x2_ref, y1_ref, out_ref, y2_ref, swap_send, swap_recv, *scratch):
+def reduce_kernel(dims, h_ref, x2_ref, y1_ref, out_ref, y2_ref, swap_send, swap_recv, xs, xsem, early,
+                  *scratch):
     halves = [scratch[:11], scratch[11:]]
     at, core = place(dims)
     depth = dims[2]
@@ -379,10 +390,20 @@
     parts = y1_ref.shape[0]
     width = y1_ref.shape[2]
     other = target(dims, at, 1 - core)
+    def loads(zz):
+        own = pl.multiple_of((2 * zz + core) * rows, rows)
+        theirs = pl.multiple_of(zz * rows, rows)
+        return (pltpu.make_async_copy(h_ref.at[:, pl.ds(own, rows)], xs.at[0, zz], xsem.at[0, zz]),
+                pltpu.make_async_copy(x2_ref.at[:, pl.ds(theirs, rows)], xs.at[1, zz], xsem.at[1, zz]))
+
+    @pl.loop(1, depth + 1)
+    def _(step):
+        for load in loads((at[2] + step) % depth):
+            load.start()
+
     greet(all_peers(dims, at, core))
     swap = send(y1_ref, y2_ref, swap_send, swap_recv, other)
     swap.start()
-    swap.wait()
 
     def first_copy(h, k1, zz):
         d1 = ORDER[h][0]
@@ -405,12 +426,15 @@
         return send(part.at[zz, at[d1], at[d2]], r3.at[k - 1], s3.at[k - 1], q3.at[k - 1],
                     target(dims, at, core, 2, k))
 
-    def compute(step):
+    def compute(step, peeled=False):
         zz = (at[2] + step) % depth
-        x1 = x1_ref[:, pl.ds(pl.multiple_of((2 * zz + core) * rows, rows), rows)]
-        x2 = x2_ref[:, pl.ds(pl.multiple_of(zz * rows, rows), rows)]
+        own, theirs = loads(zz)
+        if not peeled:
+            own.wait()
+        theirs.wait()
         for part in range(parts):
-            r = (mm(x1, y1_ref[part], TN) + mm(x2, y2_ref[part], TN)).astype(jnp.bfloat16)
+            first = early[part] if peeled else mm(xs[0, zz], y1_ref[part], TN)
+            r = (first + mm(xs[1, zz], y2_ref[part], TN)).astype(jnp.bfloat16)
             for i in range(width // cols):
                 dp = part * (width // cols) + i
                 where = (dp // dims[1], dp % dims[1])
@@ -457,10 +481,13 @@
             halves[h][0][zz, at[d1], at[d2]] = keep2(h, zz).astype(jnp.bfloat16)
             third_copy(h, step).start()
 
-    @pl.loop(1, 3)
-    def _(step):
-        compute(step)
-
+    start = (at[2] + 1) % depth
+    loads(start)[0].wait()
+    for part in range(parts):
+        early[part] = mm(xs[0, start], y1_ref[part], TN)
+    swap.wait()
+    compute(1, True)
+    compute(2)
     second(1)
 
     @pl.loop(3, depth + 1)
@@ -495,7 +522,12 @@
 
 def reduce_gradient(dims, x1, x2, y1, rows, cols):
     half = rows // 2
-    scratch = [pltpu.VMEM(y1.shape, y1.dtype), pltpu.SemaphoreType.DMA, pltpu.SemaphoreType.DMA]
+    scratch = [
+        pltpu.VMEM(y1.shape, y1.dtype), pltpu.SemaphoreType.DMA, pltpu.SemaphoreType.DMA,
+        pltpu.VMEM((2, dims[2], y1.shape[1], rows), jnp.bfloat16),
+        pltpu.SemaphoreType.DMA((2, dims[2])),
+        pltpu.VMEM((y1.shape[0], rows, y1.shape[2]), jnp.float32),
+    ]
     for h in range(2):
         n1, n2 = dims[ORDER[h][0]], dims[ORDER[h][1]]
         z = dims[2]
@@ -513,7 +545,7 @@
     return pl.pallas_call(
         functools.partial(reduce_kernel, dims),
         out_shape=jax.ShapeDtypeStruct((rows, cols), jnp.float32),
-        in_specs=[vmem] * 3,
+        in_specs=[pl.BlockSpec(memory_space=pl.ANY)] * 2 + [vmem],
         out_specs=vmem,
         scratch_shapes=scratch,
         compiler_params=pltpu.CompilerParams(
@@ -530,8 +562,8 @@
         + t_value**2 * point_end.astype(jnp.float32)
     ).astype(jnp.bfloat16)
     rows, cols = point_mid.shape
-    kv_rows, x2 = gather_project(dims, blended, hidden)
-    context, kv_grad = attend(kv_rows, queries, cotangent)
+    kv_rows, x2, cosine, sine_t = gather_project(dims, blended, hidden)
+    context, kv_grad = attend(kv_rows, queries, cotangent, cosine, sine_t)
     gradient = reduce_gradient(dims, hidden, x2, kv_grad, rows, cols)
     return (context, gradient * (2.0 * t_value * (1.0 - t_value)))
 

time: 129 us -> 120 us (0.930)
  Pallas kernels: 122 us -> 115 us
  other arithmetic: 5.83 us -> 3.83 us
    pallas_call x1, Pallas kernels: 51.6 us -> 46.8 us  [gather_project(): pl.pallas_call(body, out_shape=(jax.ShapeDtypeStruct((seq, width), jnp.bf...]
    pallas_call x1, Pallas kernels: 53.6 us -> 51.5 us  [reduce_gradient(): pl.pallas_call(functools.partial(reduce_kernel, dims), out_shape=jax.Shap...]
where the time goes in v4:
time: 120 us
  Pallas kernels  115 us (96%)
  other arithmetic  3.83 us (3%)
  between operations  1.3 us (1%)
    pallas_call x1, Pallas kernels, reduce_gradient(): pl.pallas_call(functools.partial(reduce_kernel, dims), out_shape=jax.Shap...  51.5 us
    pallas_call x1, Pallas kernels, gather_project(): pl.pallas_call(body, out_shape=(jax.ShapeDtypeStruct((seq, width), jnp.bf...  46.8 us
    pallas_call x1, Pallas kernels, attend(): pl.pallas_call(attend_kernel, grid=(heads,), out_shape=(jax.ShapeDtypeStr...  16.5 us

profile of v4, /device:TPU:0, one launch (start us, length us, event | category | flops | bytes accessed | tf_op | source)
XLA Modules:
  0.0 120.0 jit_solution(11089493311117364042)
XLA Ops:
  1.3 2.0 %add_convert_fusion.refs_0_ = bf16[512,256]{1,0:T(8,128)(2,1)} fusion(bf16[512,256]{1,0:T(8,128)(2,1)} %param.12, bf16[512,256]{1,0:T(8,128)(2,1)} %param.11, bf16[512,256]{1,0:T(8,128)(2,1)} %param.10, f32[]{:T(128)} %bitcast.2, f32[]{:T(128)} %bitcast.1, f32[]{:T(128)} %bitcast), kind=kLoop, calls=%fused_computation | loop fusion | flops 1179648 | bytes 1048588 | tf_op jit(solution)/shard_map/convert_element_type | solution.py:563
  3.2 46.8 %gather_project.1 = (bf16[512,1024]{1,0:T(8,128)(2,1)}, bf16[512,2048]{1,0:T(8,128)(2,1)}, f32[512,128]{1,0:T(8,128)}, f32[512,128]{1,0:T(8,128)}) custom-call(bf16[512,256]{1,0:T(8,128)(2,1)} %add_convert_fusion.refs_0_, bf16[512,4096]{1,0:T(8,128)(2,1)} %h_ref.1), custom_call_target="tpu_custom_call" | custom-call | tf_op jit(solution)/shard_map/gather_project/pallas_call | solution.py:356
  50.0 16.5 %attend.1 = (bf16[512,2048]{1,0:T(8,128)(2,1)}, bf16[2,512,512]{2,1,0:T(8,128)(2,1)}) custom-call(bf16[512,1024]{1,0:T(8,128)(2,1)} %get-tuple-element.8.k_ref.v_ref, bf16[512,1024]{1,0:T(8,128)(2,1)} %get-tuple-element.8.k_ref.v_ref, bf16[512,2048]{1,0:T(8,128)(2,1)} %q_ref.1, bf16[512,2048]{1,0:T(8,128)(2,1)} %g_ref.1, ...), custom_call_target="tpu_custom_call" | custom-call | tf_op jit(solution)/shard_map/attend/pallas_call | solution.py:92
  66.5 51.5 %reduce_gradient.1 = f32[512,256]{1,0:T(8,128)} custom-call(bf16[512,4096]{1,0:T(8,128)(2,1)} %h_ref.1, bf16[512,2048]{1,0:T(8,128)(2,1)} %get-tuple-element.12.x2_ref, bf16[2,512,512]{2,1,0:T(8,128)(2,1)} %get-tuple-element.13.y1_ref), custom_call_target="tpu_custom_call" | custom-call | tf_op jit(solution)/shard_map/reduce_gradient/pallas_call | solution.py:545
  118.1 1.9 %broadcast_multiply_fusion = f32[512,256]{1,0:T(8,128)} fusion(f32[512,256]{1,0:T(8,128)} %reduce_gradient.1, f32[]{:T(128)} %bitcast.1), kind=kLoop, calls=%fused_computation.1 | loop fusion | flops 131072 | bytes 1048580 | tf_op jit(solution)/shard_map/mul | solution.py:568

commit v5 on v4

--- a/solution.py
+++ b/solution.py
@@ -10,7 +10,7 @@
 
 KVH = 4
 HD = 128
-BQ = 128
+BQ = 256
 MESH = pl.DeviceIdType.MESH
 VMEM_LIMIT = 60 * 1024 * 1024
 

time: 120 us -> 120 us (level)
  no operation moved by 1% of the time
where the time goes in v5:
time: 120 us; the launch traced here: 119 us
  Pallas kernels  114 us (95%)
  other arithmetic  3.83 us (3%)
  between operations  1.3 us (1%)
    pallas_call x1, Pallas kernels, reduce_gradient(): pl.pallas_call(functools.partial(reduce_kernel, dims), out_shape=jax.Shap...  51.5 us
    pallas_call x1, Pallas kernels, gather_project(): pl.pallas_call(body, out_shape=(jax.ShapeDtypeStruct((seq, width), jnp.bf...  46.8 us
    pallas_call x1, Pallas kernels, attend(): pl.pallas_call(attend_kernel, grid=(heads,), out_shape=(jax.ShapeDtypeStr...  15.9 us

profile of v5, /device:TPU:0, one launch (start us, length us, event | category | flops | bytes accessed | tf_op | source)
XLA Modules:
  0.0 119.3 jit_solution(9836521020588678262)
XLA Ops:
  1.3 2.0 %add_convert_fusion.refs_0_ = bf16[512,256]{1,0:T(8,128)(2,1)} fusion(bf16[512,256]{1,0:T(8,128)(2,1)} %param.12, bf16[512,256]{1,0:T(8,128)(2,1)} %param.11, bf16[512,256]{1,0:T(8,128)(2,1)} %param.10, f32[]{:T(128)} %bitcast.2, f32[]{:T(128)} %bitcast.1, f32[]{:T(128)} %bitcast), kind=kLoop, calls=%fused_computation | loop fusion | flops 1179648 | bytes 1048588 | tf_op jit(solution)/shard_map/convert_element_type | solution.py:563
  3.2 46.8 %gather_project.1 = (bf16[512,1024]{1,0:T(8,128)(2,1)}, bf16[512,2048]{1,0:T(8,128)(2,1)}, f32[512,128]{1,0:T(8,128)}, f32[512,128]{1,0:T(8,128)}) custom-call(bf16[512,256]{1,0:T(8,128)(2,1)} %add_convert_fusion.refs_0_, bf16[512,4096]{1,0:T(8,128)(2,1)} %h_ref.1), custom_call_target="tpu_custom_call" | custom-call | tf_op jit(solution)/shard_map/gather_project/pallas_call | solution.py:356
  50.0 15.9 %attend.1 = (bf16[512,2048]{1,0:T(8,128)(2,1)}, bf16[2,512,512]{2,1,0:T(8,128)(2,1)}) custom-call(bf16[512,1024]{1,0:T(8,128)(2,1)} %get-tuple-element.8.k_ref.v_ref, bf16[512,1024]{1,0:T(8,128)(2,1)} %get-tuple-element.8.k_ref.v_ref, bf16[512,2048]{1,0:T(8,128)(2,1)} %q_ref.1, bf16[512,2048]{1,0:T(8,128)(2,1)} %g_ref.1, ...), custom_call_target="tpu_custom_call" | custom-call | tf_op jit(solution)/shard_map/attend/pallas_call | solution.py:92
  65.9 51.5 %reduce_gradient.1 = f32[512,256]{1,0:T(8,128)} custom-call(bf16[512,4096]{1,0:T(8,128)(2,1)} %h_ref.1, bf16[512,2048]{1,0:T(8,128)(2,1)} %get-tuple-element.12.x2_ref, bf16[2,512,512]{2,1,0:T(8,128)(2,1)} %get-tuple-element.13.y1_ref), custom_call_target="tpu_custom_call" | custom-call | tf_op jit(solution)/shard_map/reduce_gradient/pallas_call | solution.py:545
  117.5 1.9 %broadcast_multiply_fusion = f32[512,256]{1,0:T(8,128)} fusion(f32[512,256]{1,0:T(8,128)} %reduce_gradient.1, f32[]{:T(128)} %bitcast.1), kind=kLoop, calls=%fused_computation.1 | loop fusion | flops 131072 | bytes 1048580 | tf_op jit(solution)/shard_map/mul | solution.py:568
